TPU v7x, 256 devices: a whole 4x4x8 slice. The times are simulated.
256 devices in a mesh: dp: 8 (over z_hi, x), tensor: 8 (over z_lo, core), fsdp: 4 (over y).
Axes of the slice: x: 4, y: 4, z: 8 (z_hi: 2, z_lo: 4; z = z_hi * 4 + z_lo), core: 2. Of those that a mesh axis runs over, the one named last changes fastest.
Arguments:
- train_acts: bfloat16 [8192, 4096], P(('dp', 'fsdp'), 'tensor'), may hold values from -6 to 6
- val_acts: bfloat16 [8192, 4096], P(('dp', 'fsdp'), 'tensor'), may hold values from -6 to 6
- train_cot: bfloat16 [8192, 4096], P(('dp', 'fsdp'), 'tensor'), may hold values from -6 to 6
- val_cot: bfloat16 [8192, 4096], P(('dp', 'fsdp'), 'tensor'), may hold values from -6 to 6
- train_lengths: int32 [128], P(('dp', 'fsdp')), may hold values from 16 to 64
- val_lengths: int32 [128], P(('dp', 'fsdp')), may hold values from 16 to 64
- gate_weight: bfloat16 [4096, 11008], P(('dp', 'fsdp'), 'tensor'), may hold values from -0.09375 to 0.09375
- up_weight: bfloat16 [4096, 11008], P(('dp', 'fsdp'), 'tensor'), may hold values from -0.09375 to 0.09375
- in_basis: bfloat16 [11008, 64], P('tensor'), may hold values from -0.0546875 to 0.0546875
- out_basis: bfloat16 [4096, 128], P('tensor'), may hold values from -0.09375 to 0.09375
Outputs:
- scores: float32 [128, 128], P(('dp', 'fsdp'))
Inputs may be any that keep to these rules, and one draw needn't show every extreme that they name: `train_lengths`: an example's first length slots hold its tokens, the rest are padding. `val_lengths`: as for the training examples.
All inputs are finite; a program needn't handle non-finite values.
Results may differ from a plain program's by a relative error of at most 0.004.
Values may be sent and summed in bfloat16 or wider, within the bound.
A program may use at most 128 MiB of HBM per device.

v0:
```python
import jax
import jax.numpy as jnp
from jax import lax
from jax.sharding import PartitionSpec as P

SEQ = 64


def side_by_side(arrays, axis, dim, along):
    widths = [a.shape[along] for a in arrays]
    both = jnp.concatenate(arrays, axis=along)
    out = lax.all_gather(both, axis, axis=dim, tiled=True)
    return tuple(jnp.split(out, [sum(widths[:k]) for k in range(1, len(widths))], axis=along))


def from_everyone(array, axis):
    copies = jnp.broadcast_to(array, (lax.axis_size(axis), *array.shape))
    return lax.all_to_all(copies, axis, split_axis=0, concat_axis=0, tiled=True)


def taken_together(array, axis):
    return from_everyone(array, axis).sum(axis=0)


def in_blocks(array, dim, count):
    shape = array.shape
    tiles = array.reshape(*shape[:dim], count, shape[dim] // count, *shape[dim + 1 :])
    return jnp.moveaxis(tiles, dim, 0)


def summed_on_arrival(array, axis, dim):
    tiles = in_blocks(array, dim, lax.axis_size(axis))
    arrived = lax.all_to_all(tiles, axis, split_axis=0, concat_axis=0, tiled=True)
    return arrived.sum(axis=0)


def laid_out(tiles, dim):
    shape = list(tiles.shape[1:])
    shape[dim] *= tiles.shape[0]
    return jnp.moveaxis(tiles, 0, dim).reshape(shape)


def gather_directly(array, axis, dim):
    tiles = from_everyone(array, axis)
    return laid_out(tiles, dim)


def outer_sums(in_proj, out_proj, valid):
    in_three = in_proj.reshape(valid.shape[0], valid.shape[1], in_proj.shape[1]) * valid[:, :, None]
    out_three = out_proj.reshape(valid.shape[0], valid.shape[1], out_proj.shape[1])
    return jnp.einsum("esj,esk->ejk", in_three, out_three, precision=lax.Precision.HIGHEST)


def on_device(
    train_acts,
    val_acts,
    train_cot,
    val_cot,
    train_lengths,
    val_lengths,
    gate_weight,
    up_weight,
    in_basis,
    out_basis,
):
    train_full, val_full = side_by_side((train_acts, val_acts), "tensor", 1, 0)
    activations = jnp.concatenate([train_full, val_full], axis=0)
    cotangents = jnp.concatenate([train_cot, val_cot], axis=0)
    pieces = side_by_side((gate_weight, up_weight), ("dp", "fsdp"), 0, 1)
    gate_sum = jnp.dot(activations, pieces[0], preferred_element_type=jnp.float32)
    up_sum = jnp.dot(activations, pieces[1], preferred_element_type=jnp.float32)
    hidden = (jax.nn.silu(gate_sum) * up_sum).astype(jnp.bfloat16)
    in_part = jnp.dot(hidden, in_basis, preferred_element_type=jnp.float32)
    out_part = jnp.dot(cotangents, out_basis, preferred_element_type=jnp.float32)
    lengths = jnp.concatenate([train_lengths, val_lengths], axis=0)
    valid = (jnp.arange(SEQ, dtype=jnp.int32)[None, :] < lengths[:, None]).astype(jnp.float32)
    out_proj = taken_together(out_part, "tensor")
    partial_value = outer_sums(in_part, out_proj, valid)
    shares = summed_on_arrival(partial_value, "tensor", 1)
    sketch = gather_directly(shares, "tensor", 1)
    flat_sketch = sketch.reshape(sketch.shape[0], sketch.shape[1] * sketch.shape[2])
    unit_rows = flat_sketch * lax.rsqrt(
        jnp.sum(flat_sketch * flat_sketch, axis=1, keepdims=True) + 1e-06
    )
    train_count = train_lengths.shape[0]
    train_unit = unit_rows[:train_count]
    val_local = unit_rows[train_count:]
    width_all = flat_sketch.shape[1]
    share = width_all // lax.axis_size("tensor")
    first = lax.axis_index("tensor") * share
    train_share = lax.dynamic_slice_in_dim(train_unit, first, share, 1)
    val_share_local = lax.dynamic_slice_in_dim(val_local, first, share, 1)
    val_share = gather_directly(val_share_local, ("dp", "fsdp"), 0)
    partial_scores = jnp.dot(
        train_share,
        val_share.T,
        precision=lax.Precision.HIGHEST,
        preferred_element_type=jnp.float32,
    )
    product = lax.psum(partial_scores, "tensor")
    return product * jnp.sqrt(jnp.float32(width_all))


def solution(mesh):
    placed = (
        P(("dp", "fsdp"), "tensor"),
        P(("dp", "fsdp"), "tensor"),
        P(("dp", "fsdp"), "tensor"),
        P(("dp", "fsdp"), "tensor"),
        P(("dp", "fsdp")),
        P(("dp", "fsdp")),
        P(("dp", "fsdp"), "tensor"),
        P(("dp", "fsdp"), "tensor"),
        P("tensor", None),
        P("tensor", None),
    )
    return jax.shard_map(
        on_device, mesh=mesh, in_specs=placed, out_specs=P(("dp", "fsdp"), None), check_vma=False
    )
```

profile of v0, /device:TPU:1, one launch (start us, length us, event | category | flops | bytes accessed | tf_op | source)
XLA Modules:
  0.0 658.2 jit_solution(8967258331673198613)
XLA Ops:
  6.5 0.0 all-gather.3.cloned.1.call-start
  6.6 2.0 pad_maximum_fusion.1
  8.6 0.0 all-gather.3.cloned.1.call-update
  8.6 0.0 all-gather.5.cloned.1.call-start
  8.6 2.0 pad_maximum_fusion
  10.6 0.0 all-gather.5.cloned.1.call-update
  10.7 0.3 fusion.13
  11.0 0.0 copy-start.5
  11.0 1.5 broadcast_in_dim.6
  12.5 7.4 %all-to-all-start = ((f32[8,512,128]{2,1,0:T(8,128)}), f32[8,512,128]{2,1,0:T(8,128)S(1)}, u32[]{:S(2)}, u32[]{:S(2)}) async-start(f32[8,512,128]{2,1,0:T(8,128)} %broadcast_in_dim.6), calls=%async_computation | async-start | bytes 4194304 | tf_op jit(solution)/shard_map/all_to_all | solution.py:18
  19.9 0.1 pad_add_fusion
  19.9 0.1 fusion.20
  20.0 77.4 %all-to-all-done = f32[8,512,128]{2,1,0:T(8,128)S(1)} async-done(((f32[8,512,128]{2,1,0:T(8,128)}), f32[8,512,128]{2,1,0:T(8,128)S(1)}, u32[]{:S(2)}, u32[]{:S(2)}) %all-to-all-start) | async-done | bytes 2097184 | tf_op jit(solution)/shard_map/all_to_all | solution.py:18
  97.4 0.1 reduce_sum.27
  97.5 9.1 %all-gather.3.cloned.1.call-done = bf16[512,4096]{1,0:T(8,128)(2,1)} async-done(((bf16[512,512]{1,0:T(8,128)(2,1)}), bf16[512,4096]{1,0:T(8,128)(2,1)}) %all-gather.3.cloned.1.call-update) | async-done | bytes 4194320 | tf_op jit(solution)/shard_map/all_gather | solution.py:12
  106.6 453.0 %all-gather.5.cloned.1.call-done = bf16[4096,2752]{0,1:T(8,128)(2,1)} async-done(((bf16[128,2752]{0,1:T(8,128)(2,1)}), bf16[4096,2752]{0,1:T(8,128)(2,1)}) %all-gather.5.cloned.1.call-update) | async-done | bytes 22544400 | tf_op jit(solution)/shard_map/all_gather | solution.py:12
  559.7 11.2 %fusion.2 = f32[512,1376]{0,1:T(8,128)} fusion(bf16[512,4096]{1,0:T(8,128)(2,1)} %all-gather.3.cloned.1.call-done, bf16[4096,2752]{0,1:T(8,128)(2,1)} %all-gather.5.cloned.1.call-done), kind=kOutput, calls=%fused_computation.2 | convolution fusion | flops 5771362304 | bytes 18284544 | tf_op jit(solution)/shard_map/dot_general | solution.py:70
  570.9 12.9 %fusion.11 = f32[512,64]{0,1:T(8,128)S(1)} fusion(bf16[1376,64]{0,1:T(8,128)(2,1)S(1)} %copy-done, bf16[512,4096]{1,0:T(8,128)(2,1)} %all-gather.3.cloned.1.call-done, bf16[4096,2752]{0,1:T(8,128)(2,1)} %all-gather.5.cloned.1.call-done, f32[512,1376]{0,1:T(8,128)} %fusion.2), kind=kOutput, calls=%fused_computation.6 | convolution fusion | flops 5865766912 | bytes 18591744 | tf_op jit(solution)/shard_map/dot_general | solution.py:73
  583.8 0.1 reshape.40
  583.9 0.4 convolution_bitcast_fusion
  584.3 13.1 %all_to_all.20 = f32[8,8,8,128]{3,2,1,0:T(8,128)S(1)} all-to-all(f32[8,8,8,128]{3,2,1,0:T(8,128)S(1)} %bitcast.24), channel_id=1, replica_groups=mesh['dp'=8,'tensor'=8,'fsdp'=4] {'tensor'}, dimensions={0} | all-to-all | bytes 524288 | tf_op jit(solution)/shard_map/all_to_all | solution.py:33
  597.5 0.7 broadcast_in_dim.14
  598.2 4.4 all-to-all-start.2
  602.6 8.7 %all-to-all-done.2 = f32[8,8,8,128]{3,2,1,0:T(8,128)S(1)} async-done(((f32[8,8,8,128]{3,2,1,0:T(8,128)}), f32[8,8,8,128]{3,2,1,0:T(8,128)S(1)}, u32[]{:S(2)}, u32[]{:S(2)}) %all-to-all-start.2) | async-done | bytes 262176 | tf_op jit(solution)/shard_map/all_to_all | solution.py:18
  611.3 0.2 multiply_reduce_fusion
  611.4 0.2 bitcast_multiply_fusion
  611.7 0.1 broadcast_in_dim.15
  611.8 22.4 %all_to_all.21 = f32[32,4,1024]{2,1,0:T(4,128)S(1)} all-to-all(f32[32,4,1024]{2,1,0:T(4,128)S(1)} %broadcast_in_dim.15), channel_id=1, replica_groups=mesh['dp'=8,'tensor'=8,'fsdp'=4] {'dp','fsdp'}, dimensions={0} | all-to-all | bytes 1048576 | tf_op jit(solution)/shard_map/all_to_all | solution.py:18
  634.2 0.2 reshape.43
  634.3 0.5 fusion.18
  634.9 15.9 %psum.7 = f32[4,128]{1,0:T(4,128)S(1)} all-reduce(f32[4,128]{1,0:T(4,128)S(1)} %fusion.18), channel_id=1, replica_groups=mesh['dp'=8,'tensor'=8,'fsdp'=4] {'tensor'}, use_global_device_ids=true, to_apply=%region_3.4 | all-reduce | flops 512 | bytes 4096 | tf_op jit(solution)/shard_map/psum | solution.py:100
  650.8 0.6 broadcast_multiply_fusion
  (17 shorter events, 0.1 us)
Async XLA Ops:
  6.5 564.3 %copy-start = (bf16[1376,64]{0,1:T(8,128)(2,1)S(1)}, bf16[1376,64]{0,1:T(8,128)(2,1)}, u32[]{:S(2)}) copy-start(bf16[1376,64]{0,1:T(8,128)(2,1)} %param.18) | copy-start | bytes 528388
  6.5 4.1 copy-start.2
  6.5 4.1 copy-start.1
  6.5 4.1 copy-start.3
  6.5 100.1 %all-gather.3.cloned.1.call-start = ((), (), s32[]{:S(2)}) async-start(), calls=%async_computation.4 | async-start | bytes 4718592 | tf_op jit(solution)/shard_map/all_gather | solution.py:12
  8.6 551.1 %all-gather.5.cloned.1.call-start = ((), (), s32[]{:S(2)}) async-start(), calls=%async_computation.5 | async-start | bytes 23248896 | tf_op jit(solution)/shard_map/all_gather | solution.py:12
  11.0 8.9 %copy-start.4 = (s32[4]{0:T(128)S(1)}, s32[4]{0:T(128)}, u32[]{:S(2)}) copy-start(s32[4]{0:T(128)} %param.15) | copy-start | bytes 52
  11.0 8.9 %copy-start.5 = (s32[4]{0:T(128)S(1)}, s32[4]{0:T(128)}, u32[]{:S(2)}) copy-start(s32[4]{0:T(128)} %param.14) | copy-start | bytes 52
  12.5 84.9 %all-to-all-start = ((f32[8,512,128]{2,1,0:T(8,128)}), f32[8,512,128]{2,1,0:T(8,128)S(1)}, u32[]{:S(2)}, u32[]{:S(2)}) async-start(f32[8,512,128]{2,1,0:T(8,128)} %broadcast_in_dim.6), calls=%async_computation | async-start | bytes 4194304 | tf_op jit(solution)/shard_map/all_to_all | solution.py:18
  598.2 13.1 %all-to-all-start.2 = ((f32[8,8,8,128]{3,2,1,0:T(8,128)}), f32[8,8,8,128]{3,2,1,0:T(8,128)S(1)}, u32[]{:S(2)}, u32[]{:S(2)}) async-start(f32[8,8,8,128]{3,2,1,0:T(8,128)} %broadcast_in_dim.14), calls=%async_computation.2 | async-start | bytes 524288 | tf_op jit(solution)/shard_map/all_to_all | solution.py:18
Sparse Core Ops, SparseCore 0:
  9.1 97.4 all-gather.2
  109.8 449.7 all-gather.4
where the time goes:
time: 659 us; the launch traced here: 658 us
  waiting for transfers between devices  548 us (83%)
  blocking collectives  51.4 us (8%)
  matrix products  25.3 us (4%)
  between operations  13.5 us (2%)
  starting transfers between devices  11.8 us (2%)
    all_gather x2, waiting for transfers between devices, side_by_side(): out = lax.all_gather(both, axis, axis=dim, tiled=True)  462 us
    all_to_all x2, waiting for transfers between devices, from_everyone(): return lax.all_to_all(copies, axis, split_axis=0, concat_axis=0, tiled=True)  86.1 us
    all_to_all x1, blocking collectives, from_everyone(): return lax.all_to_all(copies, axis, split_axis=0, concat_axis=0, tiled=True)  22.4 us
    psum x1, blocking collectives, on_device(): product = lax.psum(partial_scores, 'tensor')  15.9 us
  transfers between devices with their start and end apart: 4, of which 4 were waited for; matrix products, arithmetic and copies ran while one was open for 1% of the time, Pallas kernels for 0%

commit v1 on v0

v1 whole, which is shorter than its diff:
```python
import jax
import jax.numpy as jnp
from jax import lax
from jax.experimental import pallas as pl
from jax.experimental.pallas import tpu as pltpu
from jax.sharding import PartitionSpec as P

SEQ = 64
MESH = pl.DeviceIdType.MESH
F32 = jnp.float32
BF16 = jnp.bfloat16
WIDE = 640
REST = 48
COLS = 1408
PLUS, MINUS = 1, -1


def mod(value, n):
    return lax.rem(value + n, n)


def body(
    tlen, vlen, gate, up, tacts, vacts, tcot, vcot, ibasis, obasis,
    out,
    wf, fx, relay, xf, acc, b2, proj, opart, orecv, osum, otr, ova,
    toward, kept, given, irecv, tbuf, vbuf, row, obuf,
    wsend, wrecv, zsend, zrecv, dsend, drecv, tsend, trecv,
):
    dp = lax.axis_index("dp")
    t = lax.axis_index("tensor")
    y = lax.axis_index("fsdp")
    zh = dp // 4
    x = lax.rem(dp, 4)
    zl = t // 2
    c = lax.rem(t, 2)
    z = zh * 4 + zl
    peer = 1 - c

    def at_z(zz, cc):
        return {"dp": (zz // 4) * 4 + x, "tensor": lax.rem(zz, 4) * 2 + cc, "fsdp": y}

    def at_xy(xx, yy):
        return {"dp": zh * 4 + xx, "tensor": t, "fsdp": yy}

    def copy(src, dst, sends, recvs, n, device):
        return pltpu.make_async_remote_copy(
            src_ref=src, dst_ref=dst, send_sem=sends.at[n], recv_sem=recvs.at[n],
            device_id=device, device_id_type=MESH,
        )

    started = []

    def start(c_):
        c_.start()
        started.append(c_)

    barrier = pltpu.get_barrier_semaphore()
    for dx in range(4):
        for dy in range(4):
            if dx or dy:
                pl.semaphore_signal(
                    barrier, inc=1, device_id=at_xy(lax.rem(x + dx, 4), lax.rem(y + dy, 4)),
                    device_id_type=MESH)
    for k in range(8):
        for cc in (c, peer):
            if k or cc is peer:
                pl.semaphore_signal(
                    barrier, inc=1, device_id=at_z(lax.rem(z + k, 8), cc), device_id_type=MESH)

    pick_r = lax.broadcasted_iota(jnp.int32, (96, 128), 0)
    pick_l = lax.broadcasted_iota(jnp.int32, (96, 128), 1)

    def pack(half):
        first = pl.multiple_of(half * WIDE, 128)
        pick_gate = (pick_l < REST) & (pick_r == pick_l + REST * half)
        pick_up = (pick_l >= 64) & (pick_l < 64 + REST) & (pick_r == pick_l - 64 + REST * half)
        rest = jnp.dot(gate[:, 1280:1376], pick_gate.astype(F32).astype(BF16), preferred_element_type=F32)
        rest += jnp.dot(up[:, 1280:1376], pick_up.astype(F32).astype(BF16), preferred_element_type=F32)
        return gate[:, pl.ds(first, WIDE)], up[:, pl.ds(first, WIDE)], rest.astype(BF16)

    fx[:, 0:WIDE], fx[:, WIDE : 2 * WIDE], fx[:, 2 * WIDE : COLS] = pack(1 - zh)
    mine = pl.ds(pl.multiple_of(y * 128, 128), 128)
    wf[dp, mine, 0:WIDE], wf[dp, mine, WIDE : 2 * WIDE], wf[dp, mine, 2 * WIDE : COLS] = pack(zh)
    pl.semaphore_wait(barrier, 30)

    def w_rows(zc, xx, yy, first, count):
        return wf.at[zc * 4 + xx, pl.ds(pl.multiple_of(yy * 128 + first, 32), count), :]

    def exchange(sign):
        n = 0 if sign == PLUS else 1
        start(copy(fx.at[pl.ds(64 * n, 64), :], relay.at[n], zsend, zrecv, n,
                   at_z(mod(z + 2 * sign, 8), c)))

    def exchange_on(sign):
        n = 0 if sign == PLUS else 1
        arrive = copy(relay.at[n], relay.at[n], zsend, zrecv, n, at_z(z, peer))
        arrive.wait_recv()
        origin = mod(z - 2 * sign, 8)
        slot = w_rows(origin // 4, x, y, 64 * n, 64)
        start(copy(relay.at[n], slot, zsend, zrecv, 2 + n, at_z(mod(z + 2 * sign, 8), c)))

    def exchanged(sign):
        n = 0 if sign == PLUS else 1
        slot = w_rows(1 - zh, x, y, 64 * n, 64)
        copy(slot, slot, zsend, zrecv, 2 + n, at_z(z, peer)).wait_recv()

    def act_slot(zz, cc, kind):
        return xf.at[lax.rem(zz, 4) * 2 + cc, zz // 4, kind]

    def kind_of(sign, n):
        return n % 2 if sign == PLUS else 1 - n % 2

    def act_send(sign, n):
        kind = kind_of(sign, n)
        base = 4 if sign == PLUS else 11
        slot = act_slot(mod(z - sign * (n // 2), 8), c, kind)
        src = slot if n > 1 else (tacts if kind == 0 else vacts)
        start(copy(src, slot, zsend, zrecv, base + n, at_z(mod(z + sign, 8), c)))

    def hand_over(slot, src, n):
        start(copy(src, slot, dsend, drecv, n, at_z(z, peer)))

    def act_arrive(sign, n):
        base = 4 if sign == PLUS else 11
        slot = act_slot(mod(z - sign * (n // 2 + 1), 8), c, kind_of(sign, n))
        copy(slot, slot, zsend, zrecv, base + n, at_z(z, peer)).wait_recv()
        if n + 2 < 7:
            act_send(sign, n + 2)
        hand_over(slot, slot, 2 + (n if sign == PLUS else 7 + n))

    def handed():
        for kind in range(2):
            slot = act_slot(z, peer, kind)
            copy(slot, slot, dsend, drecv, kind, at_z(z, peer)).wait_recv()
        for sign in (PLUS, MINUS):
            for n in range(7):
                slot = act_slot(mod(z - sign * (n // 2 + 1), 8), peer, kind_of(sign, n))
                copy(slot, slot, dsend, drecv, 2 + (n if sign == PLUS else 7 + n),
                     at_z(z, peer)).wait_recv()

    def w_part(cls, axis, da, db, part, half):
        xx, yy = (mod(x + da, 4), mod(y + db, 4)) if axis == 0 else (mod(x + db, 4), mod(y + da, 4))
        zc = zh if cls == 0 else 1 - zh
        if half is None:
            return w_rows(zc, xx, yy, 64 * part, 64)
        return w_rows(zc, xx, yy, 64 * part + 32 * half, 32)

    def w_where(cls, axis, sign, name, shift):
        first, second = axis, 1 - axis
        half = 0 if sign == PLUS else 1
        da, db, part, cut = {
            0: (0, 0, first, None), 1: (0, 0, second, None), 2: (-sign, 0, first, half),
            3: (0, -1, second, None), 4: (0, 1, second, None), 5: (0, 2, second, None),
            6: (-sign, 0, second, half), 7: (-sign, -1, second, half),
            8: (-sign, 1, second, half), 9: (-sign, 2, second, half),
        }[name]
        return w_part(cls, axis, da - shift * sign, db, part, cut)

    def w_id(cls, axis, sign, name):
        return ((cls * 2 + axis) * 2 + (0 if sign == PLUS else 1)) * 10 + name

    def w_send(cls, axis, sign, name):
        ref = w_where(cls, axis, sign, name, 0)
        to = at_xy(mod(x + sign, 4), y) if axis == 0 else at_xy(x, mod(y + sign, 4))
        start(copy(ref, ref, wsend, wrecv, w_id(cls, axis, sign, name), to))

    def w_arrive(cls, axis, sign, name):
        ref = w_where(cls, axis, sign, name, 1)
        copy(ref, ref, wsend, wrecv, w_id(cls, axis, sign, name), at_z(z, peer)).wait_recv()

    ways = [(axis, sign) for axis in (0, 1) for sign in (PLUS, MINUS)]

    def round_0(cls):
        for name in (0, 1):
            for axis, sign in ways:
                w_send(cls, axis, sign, name)

    def round_1(cls):
        for axis, sign in ways:
            w_arrive(cls, axis, sign, 0)
            w_send(cls, axis, sign, 2)
            for other in (PLUS, MINUS):
                w_send(cls, 1 - axis, other, 3 if sign == PLUS else 4)

    def round_2(cls):
        for axis, sign in ways:
            w_arrive(cls, axis, sign, 1)
            w_send(cls, axis, sign, 6)

    def round_3(cls):
        for axis in (0, 1):
            w_arrive(cls, axis, PLUS, 2)
            w_arrive(cls, axis, MINUS, 2)
            for other in (PLUS, MINUS):
                w_send(cls, 1 - axis, other, 5)

    def round_4(cls):
        for name in (3, 4):
            for axis, sign in ways:
                w_arrive(cls, axis, sign, name)
                w_send(cls, axis, sign, name + 4)

    def round_5(cls):
        for axis, sign in ways:
            w_arrive(cls, axis, sign, 5)
            w_send(cls, axis, sign, 9)

    def round_6(cls):
        for name in (6, 7, 8, 9):
            for axis, sign in ways:
                w_arrive(cls, axis, sign, name)

    exchange(PLUS)
    exchange(MINUS)
    round_0(0)
    act_send(PLUS, 0)
    act_send(MINUS, 0)
    hand_over(act_slot(z, c, 0), tacts, 0)
    hand_over(act_slot(z, c, 1), vacts, 1)
    xf[t, zh, 0] = tacts[...]
    xf[t, zh, 1] = vacts[...]

    slots = lax.broadcasted_iota(jnp.int32, (SEQ, 128), 0)
    for kind, (cot, lens) in enumerate(((tcot, tlen), (vcot, vlen))):
        value = jnp.dot(cot[...], obasis[...], preferred_element_type=F32)
        for i in range(4):
            rows = value[i * SEQ : (i + 1) * SEQ]
            opart[2 * i + kind] = jnp.where(slots < lens[i], rows, 0.0)
    dup_r = lax.broadcasted_iota(jnp.int32, (64, 128), 0)
    dup_l = lax.broadcasted_iota(jnp.int32, (64, 128), 1)
    dup = ((dup_l == dup_r) | (dup_l == dup_r + 64)).astype(F32).astype(BF16)
    main = ibasis[pl.ds(pl.multiple_of(zh * WIDE, 128), WIDE), :]
    rest = ibasis[pl.ds(pl.multiple_of(2 * WIDE + zh * REST, 16), REST), :]
    b2[0:WIDE] = jnp.dot(main, dup, preferred_element_type=F32).astype(BF16)
    b2[WIDE : WIDE + REST] = jnp.dot(rest, dup, preferred_element_type=F32).astype(BF16)
    b2[WIDE + REST : 768] = jnp.zeros((768 - WIDE - REST, 128), BF16)
    for k in range(1, 8):
        to = lax.rem(t + k, 8)
        start(copy(opart.at[to], orecv.at[t], tsend, trecv, k - 1,
                   {"dp": dp, "tensor": to, "fsdp": y}))
    orecv[t] = opart[t]

    round_1(0)
    round_2(0)
    exchange_on(PLUS)
    exchange_on(MINUS)
    act_send(PLUS, 1)
    act_send(MINUS, 1)
    round_3(0)
    for sign in (PLUS, MINUS):
        act_arrive(sign, 0)
    round_4(0)

    for k in range(1, 8):
        slot = orecv.at[mod(t - k, 8)]
        copy(slot, slot, tsend, trecv, k - 1, at_z(z, peer)).wait_recv()
    total = orecv[0]
    for k in range(1, 8):
        total += orecv[k]
    osum[...] = total
    klass = zh * 4 + zl
    train_share = copy(osum, otr, tsend, trecv, 7, at_z(z, peer))
    val_shares = []
    for zz in range(2):
        val_shares.append(copy(osum, ova, tsend, trecv, 8 + zz,
                               {"dp": zz * 4 + x, "tensor": klass, "fsdp": y}))
    own_val = [(c == 1) & (zh == zz) & (t == klass) for zz in range(2)]

    @pl.when(c == 0)
    def _():
        train_share.start()
        otr[...] = osum[...]

    for zz in range(2):
        @pl.when((c == 1) & jnp.logical_not(own_val[zz]))
        def _():
            val_shares[zz].start()

        @pl.when(own_val[zz])
        def _():
            ova[...] = osum[...]

    for sign in (PLUS, MINUS):
        act_arrive(sign, 1)
    exchanged(PLUS)
    exchanged(MINUS)
    round_0(1)
    round_5(0)
    for sign in (PLUS, MINUS):
        act_arrive(sign, 2)
    round_1(1)
    round_2(1)
    for sign in (PLUS, MINUS):
        act_arrive(sign, 3)
    round_6(0)
    round_3(1)
    for sign in (PLUS, MINUS):
        act_arrive(sign, 4)
    round_4(1)
    for sign in (PLUS, MINUS):
        act_arrive(sign, 5)
    round_5(1)
    for sign in (PLUS, MINUS):
        act_arrive(sign, 6)
    handed()
    round_6(1)

    acc[...] = jnp.zeros_like(acc)

    def step(n, carry):
        half = n // 8
        k = lax.rem(n, 8)
        a = xf[k, half].reshape(512, 512)
        acc[half] += jnp.dot(a, wf[k], preferred_element_type=F32)
        return carry

    lax.fori_loop(0, 16, step, 0)

    def silu(v):
        return v / (1.0 + jnp.exp(-v))

    def project(n, carry):
        half = n // 4
        rows = pl.ds(pl.multiple_of(lax.rem(n, 4) * 128, 128), 128)
        hidden = (silu(acc[half, rows, 0:WIDE]) * acc[half, rows, WIDE : 2 * WIDE]).astype(BF16)
        last = acc[half, rows, 2 * WIDE : COLS]
        hidden_rest = (silu(last) * pltpu.roll(last, 64, 1)).astype(BF16)
        value = jnp.dot(hidden, b2[0:WIDE], preferred_element_type=F32)
        value += jnp.dot(hidden_rest, b2[WIDE:768], preferred_element_type=F32)
        proj[half, rows, :] = value
        return carry

    lax.fori_loop(0, 8, project, 0)

    left = lax.broadcasted_iota(jnp.int32, (SEQ, 128), 1) < 64

    def message(zz, cc):
        train = proj[zz // 4, (zz % 4) * SEQ : (zz % 4 + 1) * SEQ, :]
        first = pl.multiple_of(256 + (2 * (zz % 2) + cc) * SEQ, SEQ)
        val = proj[(zz % 4) // 2, pl.ds(first, SEQ), :]
        return jnp.where(left, train, val)

    for zz in range(8):
        toward[zz] = message(zz, peer)
    start(copy(toward, given, tsend, trecv, 10, at_z(z, peer)))
    for zz in range(8):
        kept[zz] = message(zz, c)
    copy(given, given, tsend, trecv, 10, at_z(z, peer)).wait_recv()
    for zz in range(8):
        kept[zz] += given[zz]
    for k in range(1, 8):
        to = lax.rem(z + k, 8)
        start(copy(kept.at[to], irecv.at[z], tsend, trecv, 10 + k, at_z(to, c)))
    irecv[z] = kept[z]

    @pl.when(c == 1)
    def _():
        copy(otr, otr, tsend, trecv, 7, at_z(z, peer)).wait_recv()

    from_self = (zh == t // 4) & (t == lax.rem(t, 4) * 2 + 1)
    for zz in range(2):
        @pl.when((zh == zz) & jnp.logical_not(from_self))
        def _():
            copy(ova, ova, tsend, trecv, 8 + zz, at_z(z, peer)).wait_recv()

    for k in range(1, 8):
        slot = irecv.at[mod(z - k, 8)]
        copy(slot, slot, tsend, trecv, 10 + k, at_z(z, peer)).wait_recv()
    both = irecv[0]
    for k in range(1, 8):
        both += irecv[k]

    def unit(o_ref, first):
        sketch = lax.dot_general(
            both, o_ref[...], (((0,), (0,)), ((), ())),
            precision=lax.Precision.HIGHEST, preferred_element_type=F32)[first : first + 64]
        return sketch * lax.rsqrt(jnp.sum(sketch * sketch, keepdims=True) + 1e-06)

    vbuf[x * 4 + y] = unit(ova, 64).astype(BF16)
    n = 18
    for dx in range(4):
        for dy in range(4):
            if dx or dy:
                start(copy(vbuf.at[x * 4 + y], vbuf.at[x * 4 + y], tsend, trecv, n,
                           at_xy(lax.rem(x + dx, 4), lax.rem(y + dy, 4))))
                n += 1
    tbuf[zl] = unit(otr, 0)
    for k in range(1, 4):
        start(copy(tbuf.at[zl], tbuf.at[zl], tsend, trecv, 32 + k,
                   at_z(zh * 4 + lax.rem(zl + k, 4), c)))
    for k in range(1, 4):
        slot = tbuf.at[mod(zl - k, 4)]
        copy(slot, slot, tsend, trecv, 32 + k, at_z(z, peer)).wait_recv()
    n = 18
    for dx in range(4):
        for dy in range(4):
            if dx or dy:
                slot = vbuf.at[mod(x - dx, 4) * 4 + mod(y - dy, 4)]
                copy(slot, slot, tsend, trecv, n, at_z(z, peer)).wait_recv()
                n += 1

    sums = []
    for v in range(16):
        val = vbuf[v].astype(F32)
        for i in range(4):
            sums.append(jnp.sum(tbuf[i] * val, axis=0, keepdims=True))
    sums.append(jnp.zeros((64, 128), F32))
    pairs = jnp.concatenate(sums, axis=0)
    line = jnp.sum(pairs.T, axis=0, keepdims=True)
    row[...] = jnp.broadcast_to(line, (8, 128))
    for k in range(1, 8):
        to = lax.rem(t + k, 8)
        start(copy(row, obuf.at[t], tsend, trecv, 35 + k, {"dp": dp, "tensor": to, "fsdp": y}))
    obuf[t] = row[...]
    for k in range(1, 8):
        slot = obuf.at[mod(t - k, 8)]
        copy(slot, slot, tsend, trecv, 35 + k, at_z(z, peer)).wait_recv()
    out[...] = obuf[...]

    for c_ in started:
        c_.wait_send()

    @pl.when(c == 0)
    def _():
        train_share.wait_send()

    for zz in range(2):
        @pl.when((c == 1) & jnp.logical_not(own_val[zz]))
        def _():
            val_shares[zz].wait_send()


def on_device(
    train_acts, val_acts, train_cot, val_cot, train_lengths, val_lengths,
    gate_weight, up_weight, in_basis, out_basis,
):
    vmem = pl.BlockSpec(memory_space=pltpu.VMEM)
    smem = pl.BlockSpec(memory_space=pltpu.SMEM)
    dma = pltpu.SemaphoreType.DMA
    blocks = pl.pallas_call(
        body,
        out_shape=jax.ShapeDtypeStruct((8, 8, 128), F32),
        in_specs=[smem, smem] + [vmem] * 8,
        out_specs=vmem,
        scratch_shapes=[
            pltpu.VMEM((8, 512, COLS), BF16),
            pltpu.VMEM((128, COLS), BF16),
            pltpu.VMEM((2, 64, COLS), BF16),
            pltpu.VMEM((8, 2, 2, 256, 512), BF16),
            pltpu.VMEM((2, 512, COLS), F32),
            pltpu.VMEM((768, 128), BF16),
            pltpu.VMEM((2, 512, 128), F32),
            pltpu.VMEM((8, SEQ, 128), F32),
            pltpu.VMEM((8, SEQ, 128), F32),
            pltpu.VMEM((SEQ, 128), F32),
            pltpu.VMEM((SEQ, 128), F32),
            pltpu.VMEM((SEQ, 128), F32),
            pltpu.VMEM((8, SEQ, 128), F32),
            pltpu.VMEM((8, SEQ, 128), F32),
            pltpu.VMEM((8, SEQ, 128), F32),
            pltpu.VMEM((8, SEQ, 128), F32),
            pltpu.VMEM((4, 64, 128), F32),
            pltpu.VMEM((16, 64, 128), BF16),
            pltpu.VMEM((8, 128), F32),
            pltpu.VMEM((8, 8, 128), F32),
            dma((80,)), dma((80,)),
            dma((18,)), dma((18,)),
            dma((16,)), dma((16,)),
            dma((43,)), dma((43,)),
        ],
        compiler_params=pltpu.CompilerParams(
            collective_id=0, has_side_effects=True, vmem_limit_bytes=60 * 1024 * 1024
        ),
    )(train_lengths, val_lengths, gate_weight, up_weight, train_acts, val_acts,
      train_cot, val_cot, in_basis, out_basis)
    scores = blocks[:, 0, :64].reshape(2, 4, 16, 4)
    scores = scores.transpose(3, 0, 2, 1).reshape(4, 128)
    return scores * jnp.sqrt(jnp.float32(64 * 128))


def solution(mesh):
    rows = P(("dp", "fsdp"), "tensor")
    placed = (rows, rows, rows, rows, P(("dp", "fsdp")), P(("dp", "fsdp")), rows, rows,
              P("tensor", None), P("tensor", None))
    return jax.shard_map(
        on_device, mesh=mesh, in_specs=placed, out_specs=P(("dp", "fsdp"), None), check_vma=False
    )
```

time: 659 us -> 128 us (0.19)
  waiting for transfers between devices: 548 us -> 0 us
  Pallas kernels: 0 us -> 122 us
  blocking collectives: 51.4 us -> 0 us
  matrix products: 25.3 us -> 0 us
  between operations: 13.5 us -> 0.02 us
  starting transfers between devices: 11.8 us -> 0 us
    all_gather x2 -> x0, waiting for transfers between devices: 462 us -> none  [side_by_side(): out = lax.all_gather(both, axis, axis=dim, tiled=True)]
    pallas_call x0 -> x1, Pallas kernels: none -> 122 us  [on_device(): pl.pallas_call(body, out_shape=jax.ShapeDtypeStruct((8, 8, 128), F32), in...]
    all_to_all x2 -> x0, waiting for transfers between devices: 86.1 us -> none  [from_everyone(): return lax.all_to_all(copies, axis, split_axis=0, concat_axis=0, tiled=True)]
    all_to_all x2 -> x0, blocking collectives: 35.5 us -> none  [the longest x1 22.4 us: from_everyone(): return lax.all_to_all(copies, axis, split_axis=0, concat_axis=0, tiled=True)]
    dot_general x5 -> x0, matrix products: 25.3 us -> none  [the longest x1 12.9 us: on_device(): in_part = jnp.dot(hidden, in_basis, preferred_element_type=jnp.float32)]
    psum x1 -> x0, blocking collectives: 15.9 us -> none  [on_device(): product = lax.psum(partial_scores, 'tensor')]
    all_to_all x2 -> x0, starting transfers between devices: 11.7 us -> none  [from_everyone(): return lax.all_to_all(copies, axis, split_axis=0, concat_axis=0, tiled=True)]
  transfers between devices with their start and end apart: 4 -> 0, of which waited for: 4 -> 0; matrix products, arithmetic and copies ran while one was open for 1% -> 0% of each run, Pallas kernels for 0% -> 0%
where the time goes in v1:
time: 128 us
  Pallas kernels  122 us (95%)
  local copies, waits for them, and re-layouts  4.9 us (4%)
    pallas_call x1, Pallas kernels, on_device(): pl.pallas_call(body, out_shape=jax.ShapeDtypeStruct((8, 8, 128), F32), in...  122 us
    unnamed x7, local copies, waits for them, and re-layouts  3.79 us

profile of v1, /device:TPU:1, one launch (start us, length us, event | category | flops | bytes accessed | tf_op | source)
XLA Modules:
  0.0 127.6 jit_solution(5706345650510373983)
XLA Ops:
  0.0 0.0 copy-start
  0.0 1.9 %copy.17.ibasis = bf16[1376,64]{1,0:T(8,128)(2,1)} copy(bf16[1376,64]{0,1:T(8,128)(2,1)} %param.18) | data formatting | bytes 352256 | tf_op args[8]
  1.9 0.0 copy-done
  1.9 0.0 copy-start.1
  1.9 0.9 copy.15.gate
  2.8 0.1 copy-done.1
  2.9 0.9 copy.16.up
  3.8 121.9 %shard_map.100 = f32[8,8,128]{2,1,0:T(8,128)} custom-call(s32[4]{0:T(128)} %tlen.1, s32[4]{0:T(128)} %vlen.1, bf16[128,1376]{1,0:T(8,128)(2,1)} %copy.15.gate, bf16[128,1376]{1,0:T(8,128)(2,1)} %copy.16.up, bf16[256,512]{1,0:T(8,128)(2,1)} %tacts.1, bf16[256,512]{1,0:T(8,128)(2,1)} %vacts.1, bf16[256,512]{1,0:T(8,128)(2,1)} %tcot.1, bf16[256,512]{1,0:T(8,128)(2,1)} %vcot.1, ...), custom_call_target="tpu_custom_call" | custom-call | tf_op jit(solution)/shard_map/pallas_call | solution.py:440
  125.7 0.8 multiply_reduce_fusion
  126.5 0.1 mul.17
  126.6 0.3 copy.18
  126.9 0.7 mul.19
Async XLA Ops:
  0.0 1.9 %copy-start = (bf16[128,1376]{0,1:T(8,128)(2,1)S(1)}, bf16[128,1376]{0,1:T(8,128)(2,1)}, u32[]{:S(2)}) copy-start(bf16[128,1376]{0,1:T(8,128)(2,1)} %param.16) | copy-start | bytes 1056772
  1.9 1.0 copy-start.1

commit v2 on v1

--- a/solution.py
+++ b/solution.py
@@ -9,9 +9,9 @@
 MESH = pl.DeviceIdType.MESH
 F32 = jnp.float32
 BF16 = jnp.bfloat16
-WIDE = 640
-REST = 48
-COLS = 1408
+HALF = 688
+SPAN = 736
+CUT = 352
 PLUS, MINUS = 1, -1
 
 
@@ -22,7 +22,7 @@
 def body(
     tlen, vlen, gate, up, tacts, vacts, tcot, vcot, ibasis, obasis,
     out,
-    wf, fx, relay, xf, acc, b2, proj, opart, orecv, osum, otr, ova,
+    wf, relay, xf, acc, hbuf, proj, opart, orecv, osum, otr, ova,
     toward, kept, given, irecv, tbuf, vbuf, row, obuf,
     wsend, wrecv, zsend, zrecv, dsend, drecv, tsend, trecv,
 ):
@@ -55,53 +55,41 @@
         started.append(c_)
 
     barrier = pltpu.get_barrier_semaphore()
-    for dx in range(4):
-        for dy in range(4):
-            if dx or dy:
-                pl.semaphore_signal(
-                    barrier, inc=1, device_id=at_xy(lax.rem(x + dx, 4), lax.rem(y + dy, 4)),
-                    device_id_type=MESH)
-    for k in range(8):
-        for cc in (c, peer):
-            if k or cc is peer:
-                pl.semaphore_signal(
-                    barrier, inc=1, device_id=at_z(lax.rem(z + k, 8), cc), device_id_type=MESH)
-
-    pick_r = lax.broadcasted_iota(jnp.int32, (96, 128), 0)
-    pick_l = lax.broadcasted_iota(jnp.int32, (96, 128), 1)
-
-    def pack(half):
-        first = pl.multiple_of(half * WIDE, 128)
-        pick_gate = (pick_l < REST) & (pick_r == pick_l + REST * half)
-        pick_up = (pick_l >= 64) & (pick_l < 64 + REST) & (pick_r == pick_l - 64 + REST * half)
-        rest = jnp.dot(gate[:, 1280:1376], pick_gate.astype(F32).astype(BF16), preferred_element_type=F32)
-        rest += jnp.dot(up[:, 1280:1376], pick_up.astype(F32).astype(BF16), preferred_element_type=F32)
-        return gate[:, pl.ds(first, WIDE)], up[:, pl.ds(first, WIDE)], rest.astype(BF16)
-
-    fx[:, 0:WIDE], fx[:, WIDE : 2 * WIDE], fx[:, 2 * WIDE : COLS] = pack(1 - zh)
-    mine = pl.ds(pl.multiple_of(y * 128, 128), 128)
-    wf[dp, mine, 0:WIDE], wf[dp, mine, WIDE : 2 * WIDE], wf[dp, mine, 2 * WIDE : COLS] = pack(zh)
-    pl.semaphore_wait(barrier, 30)
-
-    def w_rows(zc, xx, yy, first, count):
-        return wf.at[zc * 4 + xx, pl.ds(pl.multiple_of(yy * 128 + first, 32), count), :]
+    near = [at_xy(mod(x + s, 4), y) for s in (1, -1)] + [at_xy(x, mod(y + s, 4)) for s in (1, -1)]
+    near += [at_z(mod(z + s, 8), c) for s in (1, -1, 2, -2)] + [at_z(z, peer)]
+    for device in near:
+        pl.semaphore_signal(barrier, inc=1, device_id=device, device_id_type=MESH)
+
+    weights = (gate, up)
+
+    def own_rows(half):
+        return pl.ds(pl.multiple_of(half * HALF, 16), HALF)
+
+    for part in range(2):
+        wf[dp, y, part * HALF : (part + 1) * HALF, :] = weights[part][own_rows(zh), :]
+    xf[t, zh, 0] = tacts[...]
+    xf[t, zh, 1] = vacts[...]
+    pl.semaphore_wait(barrier, len(near))
+
+    def w_rows(zc, xx, yy, part, half=None):
+        first, count = {None: (0, HALF), 0: (0, CUT), 1: (CUT, HALF - CUT)}[half]
+        return wf.at[zc * 4 + xx, yy, pl.ds(part * HALF + first, count), :]
 
     def exchange(sign):
         n = 0 if sign == PLUS else 1
-        start(copy(fx.at[pl.ds(64 * n, 64), :], relay.at[n], zsend, zrecv, n,
+        start(copy(weights[n].at[own_rows(1 - zh), :], relay.at[n], zsend, zrecv, n,
                    at_z(mod(z + 2 * sign, 8), c)))
 
     def exchange_on(sign):
         n = 0 if sign == PLUS else 1
-        arrive = copy(relay.at[n], relay.at[n], zsend, zrecv, n, at_z(z, peer))
-        arrive.wait_recv()
+        copy(relay.at[n], relay.at[n], zsend, zrecv, n, at_z(z, peer)).wait_recv()
         origin = mod(z - 2 * sign, 8)
-        slot = w_rows(origin // 4, x, y, 64 * n, 64)
+        slot = w_rows(origin // 4, x, y, n)
         start(copy(relay.at[n], slot, zsend, zrecv, 2 + n, at_z(mod(z + 2 * sign, 8), c)))
 
     def exchanged(sign):
         n = 0 if sign == PLUS else 1
-        slot = w_rows(1 - zh, x, y, 64 * n, 64)
+        slot = w_rows(1 - zh, x, y, n)
         copy(slot, slot, zsend, zrecv, 2 + n, at_z(z, peer)).wait_recv()
 
     def act_slot(zz, cc, kind):
@@ -128,22 +116,26 @@
             act_send(sign, n + 2)
         hand_over(slot, slot, 2 + (n if sign == PLUS else 7 + n))
 
-    def handed():
+    def handed_own():
         for kind in range(2):
             slot = act_slot(z, peer, kind)
             copy(slot, slot, dsend, drecv, kind, at_z(z, peer)).wait_recv()
-        for sign in (PLUS, MINUS):
-            for n in range(7):
+
+    def handed(*steps):
+        for n in steps:
+            for sign in (PLUS, MINUS):
                 slot = act_slot(mod(z - sign * (n // 2 + 1), 8), peer, kind_of(sign, n))
                 copy(slot, slot, dsend, drecv, 2 + (n if sign == PLUS else 7 + n),
                      at_z(z, peer)).wait_recv()
 
+    def acts(n):
+        for sign in (PLUS, MINUS):
+            act_arrive(sign, n)
+
     def w_part(cls, axis, da, db, part, half):
         xx, yy = (mod(x + da, 4), mod(y + db, 4)) if axis == 0 else (mod(x + db, 4), mod(y + da, 4))
         zc = zh if cls == 0 else 1 - zh
-        if half is None:
-            return w_rows(zc, xx, yy, 64 * part, 64)
-        return w_rows(zc, xx, yy, 64 * part + 32 * half, 32)
+        return w_rows(zc, xx, yy, part, half)
 
     def w_where(cls, axis, sign, name, shift):
         first, second = axis, 1 - axis
@@ -161,8 +153,11 @@
 
     def w_send(cls, axis, sign, name):
         ref = w_where(cls, axis, sign, name, 0)
+        src = ref
+        if cls == 0 and name < 2:
+            src = weights[axis if name == 0 else 1 - axis].at[own_rows(zh), :]
         to = at_xy(mod(x + sign, 4), y) if axis == 0 else at_xy(x, mod(y + sign, 4))
-        start(copy(ref, ref, wsend, wrecv, w_id(cls, axis, sign, name), to))
+        start(copy(src, ref, wsend, wrecv, w_id(cls, axis, sign, name), to))
 
     def w_arrive(cls, axis, sign, name):
         ref = w_where(cls, axis, sign, name, 1)
@@ -205,10 +200,45 @@
             w_arrive(cls, axis, sign, 5)
             w_send(cls, axis, sign, 9)
 
-    def round_6(cls):
-        for name in (6, 7, 8, 9):
+    def round_6(cls, names=(6, 7, 8, 9)):
+        for name in names:
             for axis, sign in ways:
                 w_arrive(cls, axis, sign, name)
+
+    def multiply(half, k):
+        rows = jnp.concatenate([wf[k, i] for i in range(4)], axis=1)
+        acc[half] += lax.dot_general(
+            rows, xf[k, half].reshape(512, 512), (((1,), (1,)), ((), ())),
+            preferred_element_type=F32)
+
+    away = []
+    for m in range(4):
+        there = (m // 2) * 4 + 2 * zh + m % 2
+        ahead = mod(there - z, 8)
+        away.append(jnp.minimum(ahead, lax.rem(8 - ahead, 8)) * 4 + m)
+    nearest = []
+    for p in range(4):
+        pick = 0
+        for m in range(4):
+            rank = sum((away[o] < away[m]).astype(jnp.int32) for o in range(4) if o != m)
+            pick = pick + m * (rank == p).astype(jnp.int32)
+        nearest.append(pick)
+
+    def near_tasks(p):
+        def step(n, carry):
+            multiply(nearest[p] // 2, zh * 4 + 2 * lax.rem(nearest[p], 2) + n)
+            return carry
+
+        lax.fori_loop(0, 2, step, 0)
+
+    def far_tasks(first, count):
+        def step(n, carry):
+            g = n // 2
+            dx = g + (g == 2).astype(jnp.int32) - (g == 3).astype(jnp.int32)
+            multiply(lax.rem(n, 2), (1 - zh) * 4 + lax.rem(x + dx, 4))
+            return carry
+
+        lax.fori_loop(first, first + count, step, 0)
 
     exchange(PLUS)
     exchange(MINUS)
@@ -217,8 +247,7 @@
     act_send(MINUS, 0)
     hand_over(act_slot(z, c, 0), tacts, 0)
     hand_over(act_slot(z, c, 1), vacts, 1)
-    xf[t, zh, 0] = tacts[...]
-    xf[t, zh, 1] = vacts[...]
+    acc[...] = jnp.zeros_like(acc)
 
     slots = lax.broadcasted_iota(jnp.int32, (SEQ, 128), 0)
     for kind, (cot, lens) in enumerate(((tcot, tlen), (vcot, vlen))):
@@ -226,18 +255,6 @@
         for i in range(4):
             rows = value[i * SEQ : (i + 1) * SEQ]
             opart[2 * i + kind] = jnp.where(slots < lens[i], rows, 0.0)
-    dup_r = lax.broadcasted_iota(jnp.int32, (64, 128), 0)
-    dup_l = lax.broadcasted_iota(jnp.int32, (64, 128), 1)
-    dup = ((dup_l == dup_r) | (dup_l == dup_r + 64)).astype(F32).astype(BF16)
-    main = ibasis[pl.ds(pl.multiple_of(zh * WIDE, 128), WIDE), :]
-    rest = ibasis[pl.ds(pl.multiple_of(2 * WIDE + zh * REST, 16), REST), :]
-    b2[0:WIDE] = jnp.dot(main, dup, preferred_element_type=F32).astype(BF16)
-    b2[WIDE : WIDE + REST] = jnp.dot(rest, dup, preferred_element_type=F32).astype(BF16)
-    b2[WIDE + REST : 768] = jnp.zeros((768 - WIDE - REST, 128), BF16)
-    for k in range(1, 8):
-        to = lax.rem(t + k, 8)
-        start(copy(opart.at[to], orecv.at[t], tsend, trecv, k - 1,
-                   {"dp": dp, "tensor": to, "fsdp": y}))
     orecv[t] = opart[t]
 
     round_1(0)
@@ -247,9 +264,35 @@
     act_send(PLUS, 1)
     act_send(MINUS, 1)
     round_3(0)
-    for sign in (PLUS, MINUS):
-        act_arrive(sign, 0)
+    acts(0)
     round_4(0)
+    acts(1)
+    exchanged(PLUS)
+    exchanged(MINUS)
+    round_0(1)
+    round_5(0)
+    acts(2)
+    round_6(0)
+    round_1(1)
+    acts(3)
+    round_2(1)
+    handed_own()
+    handed(0, 1, 2, 3)
+    near_tasks(0)
+    round_3(1)
+    acts(4)
+    near_tasks(1)
+    round_4(1)
+    acts(5)
+    handed(4, 5)
+    for k in range(1, 8):
+        to = lax.rem(t + k, 8)
+        start(copy(opart.at[to], orecv.at[t], tsend, trecv, k - 1,
+                   {"dp": dp, "tensor": to, "fsdp": y}))
+    near_tasks(2)
+    round_5(1)
+    acts(6)
+    handed(6)
 
     for k in range(1, 8):
         slot = orecv.at[mod(t - k, 8)]
@@ -280,54 +323,30 @@
         def _():
             ova[...] = osum[...]
 
-    for sign in (PLUS, MINUS):
-        act_arrive(sign, 1)
-    exchanged(PLUS)
-    exchanged(MINUS)
-    round_0(1)
-    round_5(0)
-    for sign in (PLUS, MINUS):
-        act_arrive(sign, 2)
-    round_1(1)
-    round_2(1)
-    for sign in (PLUS, MINUS):
-        act_arrive(sign, 3)
-    round_6(0)
-    round_3(1)
-    for sign in (PLUS, MINUS):
-        act_arrive(sign, 4)
-    round_4(1)
-    for sign in (PLUS, MINUS):
-        act_arrive(sign, 5)
-    round_5(1)
-    for sign in (PLUS, MINUS):
-        act_arrive(sign, 6)
-    handed()
-    round_6(1)
-
-    acc[...] = jnp.zeros_like(acc)
-
-    def step(n, carry):
-        half = n // 8
-        k = lax.rem(n, 8)
-        a = xf[k, half].reshape(512, 512)
-        acc[half] += jnp.dot(a, wf[k], preferred_element_type=F32)
-        return carry
-
-    lax.fori_loop(0, 16, step, 0)
+    near_tasks(3)
+    round_6(1, (6,))
+    far_tasks(0, 2)
+    round_6(1, (7, 8))
+    far_tasks(2, 4)
+    round_6(1, (9,))
+    far_tasks(6, 2)
 
     def silu(v):
         return v / (1.0 + jnp.exp(-v))
 
+    basis = ibasis[:, pl.ds(pl.multiple_of(zh * 640, 128), SPAN)]
+    basis = jnp.concatenate([basis, basis], axis=0)
+    hbuf[0 : SPAN - HALF] = jnp.zeros((SPAN - HALF, 128), BF16)
+    hbuf[HALF:SPAN] = jnp.zeros((SPAN - HALF, 128), BF16)
+
     def project(n, carry):
         half = n // 4
-        rows = pl.ds(pl.multiple_of(lax.rem(n, 4) * 128, 128), 128)
-        hidden = (silu(acc[half, rows, 0:WIDE]) * acc[half, rows, WIDE : 2 * WIDE]).astype(BF16)
-        last = acc[half, rows, 2 * WIDE : COLS]
-        hidden_rest = (silu(last) * pltpu.roll(last, 64, 1)).astype(BF16)
-        value = jnp.dot(hidden, b2[0:WIDE], preferred_element_type=F32)
-        value += jnp.dot(hidden_rest, b2[WIDE:768], preferred_element_type=F32)
-        proj[half, rows, :] = value
+        first = pl.multiple_of(lax.rem(n, 4) * 128, 128)
+        tokens = pl.ds(first, 128)
+        hidden = silu(acc[half, 0:HALF, tokens]) * acc[half, HALF : 2 * HALF, tokens]
+        hbuf[pl.ds(pl.multiple_of(zh * (SPAN - HALF), 16), HALF), :] = hidden.astype(BF16)
+        value = jnp.dot(basis, hbuf[...], preferred_element_type=F32)
+        proj[half, tokens, :] = value.T
         return carry
 
     lax.fori_loop(0, 8, project, 0)
@@ -399,15 +418,18 @@
                 copy(slot, slot, tsend, trecv, n, at_z(z, peer)).wait_recv()
                 n += 1
 
-    sums = []
-    for v in range(16):
-        val = vbuf[v].astype(F32)
-        for i in range(4):
-            sums.append(jnp.sum(tbuf[i] * val, axis=0, keepdims=True))
-    sums.append(jnp.zeros((64, 128), F32))
-    pairs = jnp.concatenate(sums, axis=0)
-    line = jnp.sum(pairs.T, axis=0, keepdims=True)
-    row[...] = jnp.broadcast_to(line, (8, 128))
+    where_r = lax.broadcasted_iota(jnp.int32, (16, 128), 0)
+    where_l = lax.broadcasted_iota(jnp.int32, (16, 128), 1)
+    place = where_l == where_r * 4 + (t // 4) * 64 + lax.rem(t, 4)
+    vals = [vbuf[v].astype(F32) for v in range(16)]
+    lines = []
+    for i in range(4):
+        train = tbuf[i]
+        pairs = jnp.concatenate(
+            [jnp.sum(train * val, axis=0, keepdims=True) for val in vals], axis=0)
+        dots = jnp.sum(pairs, axis=1, keepdims=True) * jnp.sqrt(jnp.float32(64 * 128))
+        lines.append(jnp.sum(jnp.where(place, dots, 0.0), axis=0, keepdims=True))
+    row[...] = jnp.concatenate(lines + [jnp.zeros((4, 128), F32)], axis=0)
     for k in range(1, 8):
         to = lax.rem(t + k, 8)
         start(copy(row, obuf.at[t], tsend, trecv, 35 + k, {"dp": dp, "tensor": to, "fsdp": y}))
@@ -415,7 +437,10 @@
     for k in range(1, 8):
         slot = obuf.at[mod(t - k, 8)]
         copy(slot, slot, tsend, trecv, 35 + k, at_z(z, peer)).wait_recv()
-    out[...] = obuf[...]
+    scores = obuf[0]
+    for k in range(1, 8):
+        scores += obuf[k]
+    out[...] = scores[0:4]
 
     for c_ in started:
         c_.wait_send()
@@ -437,18 +462,17 @@
     vmem = pl.BlockSpec(memory_space=pltpu.VMEM)
     smem = pl.BlockSpec(memory_space=pltpu.SMEM)
     dma = pltpu.SemaphoreType.DMA
-    blocks = pl.pallas_call(
+    return pl.pallas_call(
         body,
-        out_shape=jax.ShapeDtypeStruct((8, 8, 128), F32),
+        out_shape=jax.ShapeDtypeStruct((4, 128), F32),
         in_specs=[smem, smem] + [vmem] * 8,
         out_specs=vmem,
         scratch_shapes=[
-            pltpu.VMEM((8, 512, COLS), BF16),
-            pltpu.VMEM((128, COLS), BF16),
-            pltpu.VMEM((2, 64, COLS), BF16),
+            pltpu.VMEM((8, 4, 2 * HALF, 128), BF16),
+            pltpu.VMEM((2, HALF, 128), BF16),
             pltpu.VMEM((8, 2, 2, 256, 512), BF16),
-            pltpu.VMEM((2, 512, COLS), F32),
-            pltpu.VMEM((768, 128), BF16),
+            pltpu.VMEM((2, 2 * HALF, 512), F32),
+            pltpu.VMEM((SPAN, 128), BF16),
             pltpu.VMEM((2, 512, 128), F32),
             pltpu.VMEM((8, SEQ, 128), F32),
             pltpu.VMEM((8, SEQ, 128), F32),
@@ -471,11 +495,8 @@
         compiler_params=pltpu.CompilerParams(
             collective_id=0, has_side_effects=True, vmem_limit_bytes=60 * 1024 * 1024
         ),
-    )(train_lengths, val_lengths, gate_weight, up_weight, train_acts, val_acts,
-      train_cot, val_cot, in_basis, out_basis)
-    scores = blocks[:, 0, :64].reshape(2, 4, 16, 4)
-    scores = scores.transpose(3, 0, 2, 1).reshape(4, 128)
-    return scores * jnp.sqrt(jnp.float32(64 * 128))
+    )(train_lengths, val_lengths, gate_weight.T, up_weight.T, train_acts, val_acts,
+      train_cot, val_cot, in_basis.T, out_basis)
 
 
 def solution(mesh):

time: 128 us -> 113 us (0.88)
  Pallas kernels: 122 us -> 111 us
  local copies, waits for them, and re-layouts: 4.9 us -> 1.26 us
    pallas_call x1, Pallas kernels: 122 us -> 111 us  [on_device(): pl.pallas_call(body, out_shape=jax.ShapeDtypeStruct((4, 128), F32), in_sp...]
    unnamed x7 -> x1, local copies, waits for them, and re-layouts: 3.79 us -> 1.26 us
where the time goes in v2:
time: 113 us
  Pallas kernels  111 us (98%)
  local copies, waits for them, and re-layouts  1.26 us (1%)
    pallas_call x1, Pallas kernels, on_device(): pl.pallas_call(body, out_shape=jax.ShapeDtypeStruct((4, 128), F32), in_sp...  111 us

profile of v2, /device:TPU:1, one launch (start us, length us, event | category | flops | bytes accessed | tf_op | source)
XLA Modules:
  0.0 112.6 jit_solution(17906393949356602783)
XLA Ops:
  0.0 111.3 %shard_map.100 = f32[4,128]{1,0:T(4,128)} custom-call(s32[4]{0:T(128)} %tlen.1, s32[4]{0:T(128)} %vlen.1, bf16[1376,128]{1,0:T(8,128)(2,1)} %bitcast.3, bf16[1376,128]{1,0:T(8,128)(2,1)} %bitcast.4, bf16[256,512]{1,0:T(8,128)(2,1)} %tacts.1, bf16[256,512]{1,0:T(8,128)(2,1)} %vacts.1, bf16[256,512]{1,0:T(8,128)(2,1)} %tcot.1, bf16[256,512]{1,0:T(8,128)(2,1)} %vcot.1, ...), custom_call_target="tpu_custom_call" | custom-call | tf_op jit(solution)/shard_map/pallas_call | solution.py:465
  111.3 1.3 %copy.12 = f32[4,128]{1,0:T(4,128)} copy(f32[4,128]{1,0:T(4,128)} %shard_map.100) | data formatting | bytes 4096

commit v3 on v2

--- a/solution.py
+++ b/solution.py
@@ -20,11 +20,11 @@
 
 
 def body(
-    tlen, vlen, gate, up, tacts, vacts, tcot, vcot, ibasis, obasis,
+    tlen_in, vlen_in, gate, up, tacts, vacts, tcot, vcot, ibasis_in, obasis_in,
     out,
-    wf, relay, xf, acc, hbuf, proj, opart, orecv, osum, otr, ova,
+    tlen, vlen, other, cots, ibasis, obasis, wf, relay, xf, acc, hbuf, proj, opart, orecv, osum, otr, ova,
     toward, kept, given, irecv, tbuf, vbuf, row, obuf,
-    wsend, wrecv, zsend, zrecv, dsend, drecv, tsend, trecv,
+    wsend, wrecv, zsend, zrecv, dsend, drecv, tsend, trecv, isem,
 ):
     dp = lax.axis_index("dp")
     t = lax.axis_index("tensor")
@@ -60,15 +60,22 @@
     for device in near:
         pl.semaphore_signal(barrier, inc=1, device_id=device, device_id_type=MESH)
 
-    weights = (gate, up)
-
     def own_rows(half):
         return pl.ds(pl.multiple_of(half * HALF, 16), HALF)
 
-    for part in range(2):
-        wf[dp, y, part * HALF : (part + 1) * HALF, :] = weights[part][own_rows(zh), :]
-    xf[t, zh, 0] = tacts[...]
-    xf[t, zh, 1] = vacts[...]
+    fetches = [
+        (gate.at[own_rows(zh), :], wf.at[dp, y, pl.ds(0, HALF), :]),
+        (up.at[own_rows(zh), :], wf.at[dp, y, pl.ds(HALF, HALF), :]),
+        (gate.at[own_rows(1 - zh), :], other.at[0]), (up.at[own_rows(1 - zh), :], other.at[1]),
+        (tacts, xf.at[t, zh, 0]), (vacts, xf.at[t, zh, 1]),
+        (tcot, cots.at[0]), (vcot, cots.at[1]), (obasis_in, obasis), (ibasis_in, ibasis),
+        (tlen_in, tlen), (vlen_in, vlen),
+    ]
+    fetches = [pltpu.make_async_copy(a, b, isem.at[n]) for n, (a, b) in enumerate(fetches)]
+    for fetch in fetches:
+        fetch.start()
+    for fetch in fetches[:6]:
+        fetch.wait()
     pl.semaphore_wait(barrier, len(near))
 
     def w_rows(zc, xx, yy, part, half=None):
@@ -77,7 +84,7 @@
 
     def exchange(sign):
         n = 0 if sign == PLUS else 1
-        start(copy(weights[n].at[own_rows(1 - zh), :], relay.at[n], zsend, zrecv, n,
+        start(copy(other.at[n], relay.at[n], zsend, zrecv, n,
                    at_z(mod(z + 2 * sign, 8), c)))
 
     def exchange_on(sign):
@@ -102,11 +109,10 @@
         kind = kind_of(sign, n)
         base = 4 if sign == PLUS else 11
         slot = act_slot(mod(z - sign * (n // 2), 8), c, kind)
-        src = slot if n > 1 else (tacts if kind == 0 else vacts)
-        start(copy(src, slot, zsend, zrecv, base + n, at_z(mod(z + sign, 8), c)))
-
-    def hand_over(slot, src, n):
-        start(copy(src, slot, dsend, drecv, n, at_z(z, peer)))
+        start(copy(slot, slot, zsend, zrecv, base + n, at_z(mod(z + sign, 8), c)))
+
+    def hand_over(slot, n):
+        start(copy(slot, slot, dsend, drecv, n, at_z(z, peer)))
 
     def act_arrive(sign, n):
         base = 4 if sign == PLUS else 11
@@ -114,7 +120,7 @@
         copy(slot, slot, zsend, zrecv, base + n, at_z(z, peer)).wait_recv()
         if n + 2 < 7:
             act_send(sign, n + 2)
-        hand_over(slot, slot, 2 + (n if sign == PLUS else 7 + n))
+        hand_over(slot, 2 + (n if sign == PLUS else 7 + n))
 
     def handed_own():
         for kind in range(2):
@@ -153,11 +159,8 @@
 
     def w_send(cls, axis, sign, name):
         ref = w_where(cls, axis, sign, name, 0)
-        src = ref
-        if cls == 0 and name < 2:
-            src = weights[axis if name == 0 else 1 - axis].at[own_rows(zh), :]
         to = at_xy(mod(x + sign, 4), y) if axis == 0 else at_xy(x, mod(y + sign, 4))
-        start(copy(src, ref, wsend, wrecv, w_id(cls, axis, sign, name), to))
+        start(copy(ref, ref, wsend, wrecv, w_id(cls, axis, sign, name), to))
 
     def w_arrive(cls, axis, sign, name):
         ref = w_where(cls, axis, sign, name, 1)
@@ -245,13 +248,15 @@
     round_0(0)
     act_send(PLUS, 0)
     act_send(MINUS, 0)
-    hand_over(act_slot(z, c, 0), tacts, 0)
-    hand_over(act_slot(z, c, 1), vacts, 1)
+    hand_over(act_slot(z, c, 0), 0)
+    hand_over(act_slot(z, c, 1), 1)
     acc[...] = jnp.zeros_like(acc)
 
+    for fetch in fetches[6:]:
+        fetch.wait()
     slots = lax.broadcasted_iota(jnp.int32, (SEQ, 128), 0)
-    for kind, (cot, lens) in enumerate(((tcot, tlen), (vcot, vlen))):
-        value = jnp.dot(cot[...], obasis[...], preferred_element_type=F32)
+    for kind, lens in enumerate((tlen, vlen)):
+        value = jnp.dot(cots[kind], obasis[...], preferred_element_type=F32)
         for i in range(4):
             rows = value[i * SEQ : (i + 1) * SEQ]
             opart[2 * i + kind] = jnp.where(slots < lens[i], rows, 0.0)
@@ -294,6 +299,12 @@
     acts(6)
     handed(6)
 
+    near_tasks(3)
+    round_6(1, (6,))
+    far_tasks(0, 2)
+    round_6(1, (7, 8))
+    far_tasks(2, 4)
+
     for k in range(1, 8):
         slot = orecv.at[mod(t - k, 8)]
         copy(slot, slot, tsend, trecv, k - 1, at_z(z, peer)).wait_recv()
@@ -323,33 +334,40 @@
         def _():
             ova[...] = osum[...]
 
-    near_tasks(3)
-    round_6(1, (6,))
-    far_tasks(0, 2)
-    round_6(1, (7, 8))
-    far_tasks(2, 4)
     round_6(1, (9,))
-    far_tasks(6, 2)
+    far_tasks(6, 1)
 
     def silu(v):
         return v / (1.0 + jnp.exp(-v))
 
     basis = ibasis[:, pl.ds(pl.multiple_of(zh * 640, 128), SPAN)]
     basis = jnp.concatenate([basis, basis], axis=0)
-    hbuf[0 : SPAN - HALF] = jnp.zeros((SPAN - HALF, 128), BF16)
-    hbuf[HALF:SPAN] = jnp.zeros((SPAN - HALF, 128), BF16)
-
-    def project(n, carry):
-        half = n // 4
-        first = pl.multiple_of(lax.rem(n, 4) * 128, 128)
-        tokens = pl.ds(first, 128)
+    hbuf[0 : SPAN - HALF] = jnp.zeros((SPAN - HALF, 256), BF16)
+    hbuf[HALF:SPAN] = jnp.zeros((SPAN - HALF, 256), BF16)
+
+    def project(half, n):
+        tokens = pl.ds(pl.multiple_of(n * 256, 256), 256)
         hidden = silu(acc[half, 0:HALF, tokens]) * acc[half, HALF : 2 * HALF, tokens]
         hbuf[pl.ds(pl.multiple_of(zh * (SPAN - HALF), 16), HALF), :] = hidden.astype(BF16)
         value = jnp.dot(basis, hbuf[...], preferred_element_type=F32)
         proj[half, tokens, :] = value.T
+
+    def last_task(n, carry):
+        k = (1 - zh) * 4 + lax.rem(x + 2, 4)
+        rows = jnp.concatenate([wf[k, i] for i in range(4)], axis=1)
+        tokens = pl.ds(pl.multiple_of(n * 256, 256), 256)
+        acc[1, :, tokens] += lax.dot_general(
+            rows, xf[k, 1, n], (((1,), (1,)), ((), ())), preferred_element_type=F32)
+        project(0, n)
         return carry
 
-    lax.fori_loop(0, 8, project, 0)
+    lax.fori_loop(0, 2, last_task, 0)
+
+    def last_half(n, carry):
+        project(1, n)
+        return carry
+
+    lax.fori_loop(0, 2, last_half, 0)
 
     left = lax.broadcasted_iota(jnp.int32, (SEQ, 128), 1) < 64
 
@@ -460,19 +478,24 @@
     gate_weight, up_weight, in_basis, out_basis,
 ):
     vmem = pl.BlockSpec(memory_space=pltpu.VMEM)
-    smem = pl.BlockSpec(memory_space=pltpu.SMEM)
     dma = pltpu.SemaphoreType.DMA
     return pl.pallas_call(
         body,
         out_shape=jax.ShapeDtypeStruct((4, 128), F32),
-        in_specs=[smem, smem] + [vmem] * 8,
+        in_specs=[pl.BlockSpec(memory_space=pl.ANY)] * 10,
         out_specs=vmem,
         scratch_shapes=[
+            pltpu.SMEM((4,), jnp.int32),
+            pltpu.SMEM((4,), jnp.int32),
+            pltpu.VMEM((2, HALF, 128), BF16),
+            pltpu.VMEM((2, 256, 512), BF16),
+            pltpu.VMEM((64, 1376), BF16),
+            pltpu.VMEM((512, 128), BF16),
             pltpu.VMEM((8, 4, 2 * HALF, 128), BF16),
             pltpu.VMEM((2, HALF, 128), BF16),
             pltpu.VMEM((8, 2, 2, 256, 512), BF16),
             pltpu.VMEM((2, 2 * HALF, 512), F32),
-            pltpu.VMEM((SPAN, 128), BF16),
+            pltpu.VMEM((SPAN, 256), BF16),
             pltpu.VMEM((2, 512, 128), F32),
             pltpu.VMEM((8, SEQ, 128), F32),
             pltpu.VMEM((8, SEQ, 128), F32),
@@ -491,6 +514,7 @@
             dma((18,)), dma((18,)),
             dma((16,)), dma((16,)),
             dma((43,)), dma((43,)),
+            dma((12,)),
         ],
         compiler_params=pltpu.CompilerParams(
             collective_id=0, has_side_effects=True, vmem_limit_bytes=60 * 1024 * 1024

time: 113 us -> 106 us (0.938)
  Pallas kernels: 111 us -> 105 us
    pallas_call x1, Pallas kernels: 111 us -> 105 us  [on_device(): pl.pallas_call(body, out_shape=jax.ShapeDtypeStruct((4, 128), F32), in_sp...]
where the time goes in v3:
time: 106 us
  Pallas kernels  105 us (99%)
  local copies, waits for them, and re-layouts  1.26 us (1%)
    pallas_call x1, Pallas kernels, on_device(): pl.pallas_call(body, out_shape=jax.ShapeDtypeStruct((4, 128), F32), in_sp...  105 us

profile of v3, /device:TPU:1, one launch (start us, length us, event | category | flops | bytes accessed | tf_op | source)
XLA Modules:
  0.0 106.2 jit_solution(12592801866899177615)
XLA Ops:
  0.0 104.9 %shard_map.100 = f32[4,128]{1,0:T(4,128)} custom-call(s32[4]{0:T(128)} %tlen_in.1, s32[4]{0:T(128)} %vlen_in.1, bf16[1376,128]{1,0:T(8,128)(2,1)} %bitcast.3, bf16[1376,128]{1,0:T(8,128)(2,1)} %bitcast.4, bf16[256,512]{1,0:T(8,128)(2,1)} %tacts.1, bf16[256,512]{1,0:T(8,128)(2,1)} %vacts.1, bf16[256,512]{1,0:T(8,128)(2,1)} %tcot.1, bf16[256,512]{1,0:T(8,128)(2,1)} %vcot.1, ...), custom_call_target="tpu_custom_call" | custom-call | tf_op jit(solution)/shard_map/pallas_call | solution.py:482
  104.9 1.3 %copy.12 = f32[4,128]{1,0:T(4,128)} copy(f32[4,128]{1,0:T(4,128)} %shard_map.100) | data formatting | bytes 4096

commit v4 on v3

--- a/solution.py
+++ b/solution.py
@@ -23,7 +23,7 @@
     tlen_in, vlen_in, gate, up, tacts, vacts, tcot, vcot, ibasis_in, obasis_in,
     out,
     tlen, vlen, other, cots, ibasis, obasis, wf, relay, xf, acc, hbuf, proj, opart, orecv, osum, otr, ova,
-    toward, kept, given, irecv, tbuf, vbuf, row, obuf,
+    toward, kept, given, passed, irecv, tbuf, vbuf, row, obuf,
     wsend, wrecv, zsend, zrecv, dsend, drecv, tsend, trecv, isem,
 ):
     dp = lax.axis_index("dp")
@@ -243,6 +243,12 @@
 
         lax.fori_loop(first, first + count, step, 0)
 
+    def gap(half):
+        ahead = mod(half * 4 + 2 * (1 - zh) + x // 2 - z, 8)
+        return jnp.minimum(ahead, lax.rem(8 - ahead, 8))
+
+    nearer = (gap(1) < gap(0)).astype(jnp.int32)
+
     exchange(PLUS)
     exchange(MINUS)
     round_0(0)
@@ -271,15 +277,15 @@
     round_3(0)
     acts(0)
     round_4(0)
-    acts(1)
     exchanged(PLUS)
     exchanged(MINUS)
     round_0(1)
+    acts(1)
     round_5(0)
     acts(2)
-    round_6(0)
     round_1(1)
     acts(3)
+    round_6(0)
     round_2(1)
     handed_own()
     handed(0, 1, 2, 3)
@@ -288,22 +294,29 @@
     acts(4)
     near_tasks(1)
     round_4(1)
+    for sign in (PLUS, MINUS):
+        w_arrive(1, 1, sign, 6)
+    multiply(nearer, (1 - zh) * 4 + x)
     acts(5)
     handed(4, 5)
-    for k in range(1, 8):
-        to = lax.rem(t + k, 8)
-        start(copy(opart.at[to], orecv.at[t], tsend, trecv, k - 1,
-                   {"dp": dp, "tensor": to, "fsdp": y}))
     near_tasks(2)
     round_5(1)
     acts(6)
     handed(6)
+    for k in range(1, 8):
+        to = lax.rem(t + k, 8)
+        start(copy(opart.at[to], orecv.at[t], tsend, trecv, k - 1,
+                   {"dp": dp, "tensor": to, "fsdp": y}))
 
     near_tasks(3)
-    round_6(1, (6,))
-    far_tasks(0, 2)
+    multiply(1 - nearer, (1 - zh) * 4 + x)
+    for sign in (PLUS, MINUS):
+        w_arrive(1, 0, sign, 6)
     round_6(1, (7, 8))
     far_tasks(2, 4)
+
+    round_6(1, (9,))
+    far_tasks(6, 1)
 
     for k in range(1, 8):
         slot = orecv.at[mod(t - k, 8)]
@@ -334,9 +347,6 @@
         def _():
             ova[...] = osum[...]
 
-    round_6(1, (9,))
-    far_tasks(6, 1)
-
     def silu(v):
         return v / (1.0 + jnp.exp(-v))
 
@@ -384,11 +394,11 @@
         kept[zz] = message(zz, c)
     copy(given, given, tsend, trecv, 10, at_z(z, peer)).wait_recv()
     for zz in range(8):
-        kept[zz] += given[zz]
+        passed[zz] = (kept[zz] + given[zz]).astype(BF16)
     for k in range(1, 8):
         to = lax.rem(z + k, 8)
-        start(copy(kept.at[to], irecv.at[z], tsend, trecv, 10 + k, at_z(to, c)))
-    irecv[z] = kept[z]
+        start(copy(passed.at[to], irecv.at[z], tsend, trecv, 10 + k, at_z(to, c)))
+    both = kept[z] + given[z]
 
     @pl.when(c == 1)
     def _():
@@ -403,9 +413,8 @@
     for k in range(1, 8):
         slot = irecv.at[mod(z - k, 8)]
         copy(slot, slot, tsend, trecv, 10 + k, at_z(z, peer)).wait_recv()
-    both = irecv[0]
-    for k in range(1, 8):
-        both += irecv[k]
+    for k in range(1, 8):
+        both += irecv[mod(z - k, 8)].astype(F32)
 
     def unit(o_ref, first):
         sketch = lax.dot_general(
@@ -436,16 +445,22 @@
                 copy(slot, slot, tsend, trecv, n, at_z(z, peer)).wait_recv()
                 n += 1
 
-    where_r = lax.broadcasted_iota(jnp.int32, (16, 128), 0)
-    where_l = lax.broadcasted_iota(jnp.int32, (16, 128), 1)
-    place = where_l == where_r * 4 + (t // 4) * 64 + lax.rem(t, 4)
-    vals = [vbuf[v].astype(F32) for v in range(16)]
+    where_r = lax.broadcasted_iota(jnp.int32, (128, 128), 0)
+    where_l = lax.broadcasted_iota(jnp.int32, (128, 128), 1)
+    place = where_l == (where_r // 8) * 4 + (t // 4) * 64 + lax.rem(t, 4)
+    blocks = [[] for _ in range(4)]
+    for v in range(16):
+        val = vbuf[v].astype(F32)
+        for i in range(4):
+            product = tbuf[i] * val
+            parts = [product[8 * q : 8 * q + 8] for q in range(8)]
+            while len(parts) > 1:
+                parts = [parts[q] + parts[q + 1] for q in range(0, len(parts), 2)]
+            blocks[i].append(parts[0])
     lines = []
     for i in range(4):
-        train = tbuf[i]
-        pairs = jnp.concatenate(
-            [jnp.sum(train * val, axis=0, keepdims=True) for val in vals], axis=0)
-        dots = jnp.sum(pairs, axis=1, keepdims=True) * jnp.sqrt(jnp.float32(64 * 128))
+        dots = jnp.sum(jnp.concatenate(blocks[i], axis=0), axis=1, keepdims=True)
+        dots = dots * jnp.sqrt(jnp.float32(64 * 128))
         lines.append(jnp.sum(jnp.where(place, dots, 0.0), axis=0, keepdims=True))
     row[...] = jnp.concatenate(lines + [jnp.zeros((4, 128), F32)], axis=0)
     for k in range(1, 8):
@@ -505,7 +520,8 @@
             pltpu.VMEM((8, SEQ, 128), F32),
             pltpu.VMEM((8, SEQ, 128), F32),
             pltpu.VMEM((8, SEQ, 128), F32),
-            pltpu.VMEM((8, SEQ, 128), F32),
+            pltpu.VMEM((8, SEQ, 128), BF16),
+            pltpu.VMEM((8, SEQ, 128), BF16),
             pltpu.VMEM((4, 64, 128), F32),
             pltpu.VMEM((16, 64, 128), BF16),
             pltpu.VMEM((8, 128), F32),

time: 106 us -> 99.7 us (0.941)
  Pallas kernels: 105 us -> 98.3 us
    pallas_call x1, Pallas kernels: 105 us -> 98.3 us  [on_device(): pl.pallas_call(body, out_shape=jax.ShapeDtypeStruct((4, 128), F32), in_sp...]
where the time goes in v4:
time: 99.7 us; the launch traced here: 99.6 us
  Pallas kernels  98.3 us (99%)
  local copies, waits for them, and re-layouts  1.26 us (1%)
    pallas_call x1, Pallas kernels, on_device(): pl.pallas_call(body, out_shape=jax.ShapeDtypeStruct((4, 128), F32), in_sp...  98.3 us

profile of v4, /device:TPU:1, one launch (start us, length us, event | category | flops | bytes accessed | tf_op | source)
XLA Modules:
  0.0 99.6 jit_solution(7402222931602708419)
XLA Ops:
  0.0 98.3 %shard_map.100 = f32[4,128]{1,0:T(4,128)} custom-call(s32[4]{0:T(128)} %tlen_in.1, s32[4]{0:T(128)} %vlen_in.1, bf16[1376,128]{1,0:T(8,128)(2,1)} %bitcast.3, bf16[1376,128]{1,0:T(8,128)(2,1)} %bitcast.4, bf16[256,512]{1,0:T(8,128)(2,1)} %tacts.1, bf16[256,512]{1,0:T(8,128)(2,1)} %vacts.1, bf16[256,512]{1,0:T(8,128)(2,1)} %tcot.1, bf16[256,512]{1,0:T(8,128)(2,1)} %vcot.1, ...), custom_call_target="tpu_custom_call" | custom-call | tf_op jit(solution)/shard_map/pallas_call | solution.py:497
  98.4 1.3 %copy.12 = f32[4,128]{1,0:T(4,128)} copy(f32[4,128]{1,0:T(4,128)} %shard_map.100) | data formatting | bytes 4096

commit v5 on v4

--- a/solution.py
+++ b/solution.py
@@ -208,11 +208,11 @@
             for axis, sign in ways:
                 w_arrive(cls, axis, sign, name)
 
-    def multiply(half, k):
-        rows = jnp.concatenate([wf[k, i] for i in range(4)], axis=1)
+    def multiply(half, *ks):
+        rows = jnp.concatenate([wf[k, i] for k in ks for i in range(4)], axis=1)
+        tokens = jnp.concatenate([xf[k, half].reshape(512, 512) for k in ks], axis=1)
         acc[half] += lax.dot_general(
-            rows, xf[k, half].reshape(512, 512), (((1,), (1,)), ((), ())),
-            preferred_element_type=F32)
+            rows, tokens, (((1,), (1,)), ((), ())), preferred_element_type=F32)
 
     away = []
     for m in range(4):
@@ -228,20 +228,15 @@
         nearest.append(pick)
 
     def near_tasks(p):
-        def step(n, carry):
-            multiply(nearest[p] // 2, zh * 4 + 2 * lax.rem(nearest[p], 2) + n)
+        first = zh * 4 + 2 * lax.rem(nearest[p], 2)
+        multiply(nearest[p] // 2, first, first + 1)
+
+    def side_tasks():
+        def step(half, carry):
+            multiply(half, (1 - zh) * 4 + lax.rem(x + 1, 4), (1 - zh) * 4 + lax.rem(x + 3, 4))
             return carry
 
         lax.fori_loop(0, 2, step, 0)
-
-    def far_tasks(first, count):
-        def step(n, carry):
-            g = n // 2
-            dx = g + (g == 2).astype(jnp.int32) - (g == 3).astype(jnp.int32)
-            multiply(lax.rem(n, 2), (1 - zh) * 4 + lax.rem(x + dx, 4))
-            return carry
-
-        lax.fori_loop(first, first + count, step, 0)
 
     def gap(half):
         ahead = mod(half * 4 + 2 * (1 - zh) + x // 2 - z, 8)
@@ -313,10 +308,10 @@
     for sign in (PLUS, MINUS):
         w_arrive(1, 0, sign, 6)
     round_6(1, (7, 8))
-    far_tasks(2, 4)
+    side_tasks()
 
     round_6(1, (9,))
-    far_tasks(6, 1)
+    multiply(0, (1 - zh) * 4 + lax.rem(x + 2, 4))
 
     for k in range(1, 8):
         slot = orecv.at[mod(t - k, 8)]
@@ -395,7 +390,7 @@
     copy(given, given, tsend, trecv, 10, at_z(z, peer)).wait_recv()
     for zz in range(8):
         passed[zz] = (kept[zz] + given[zz]).astype(BF16)
-    for k in range(1, 8):
+    for k in (4, 3, 5, 2, 6, 1, 7):
         to = lax.rem(z + k, 8)
         start(copy(passed.at[to], irecv.at[z], tsend, trecv, 10 + k, at_z(to, c)))
     both = kept[z] + given[z]
@@ -423,13 +418,12 @@
         return sketch * lax.rsqrt(jnp.sum(sketch * sketch, keepdims=True) + 1e-06)
 
     vbuf[x * 4 + y] = unit(ova, 64).astype(BF16)
-    n = 18
-    for dx in range(4):
-        for dy in range(4):
-            if dx or dy:
-                start(copy(vbuf.at[x * 4 + y], vbuf.at[x * 4 + y], tsend, trecv, n,
-                           at_xy(lax.rem(x + dx, 4), lax.rem(y + dy, 4))))
-                n += 1
+    hops = [0, 1, 2, 1]
+    plane = sorted(((a, b) for a in range(4) for b in range(4)),
+                   key=lambda d: (hops[d[0]] + hops[d[1]], d))
+    for dx, dy in plane[:0:-1]:
+        start(copy(vbuf.at[x * 4 + y], vbuf.at[x * 4 + y], tsend, trecv, 17 + dx * 4 + dy,
+                   at_xy(lax.rem(x + dx, 4), lax.rem(y + dy, 4))))
     tbuf[zl] = unit(otr, 0)
     for k in range(1, 4):
         start(copy(tbuf.at[zl], tbuf.at[zl], tsend, trecv, 32 + k,

time: 99.7 us -> 99 us (level)
  no operation moved by 1% of the time
where the time goes in v5:
time: 99 us; the launch traced here: 98.9 us
  Pallas kernels  97.6 us (99%)
  local copies, waits for them, and re-layouts  1.26 us (1%)
    pallas_call x1, Pallas kernels, on_device(): pl.pallas_call(body, out_shape=jax.ShapeDtypeStruct((4, 128), F32), in_sp...  97.6 us

profile of v5, /device:TPU:1, one launch (start us, length us, event | category | flops | bytes accessed | tf_op | source)
XLA Modules:
  0.0 98.9 jit_solution(10043031384187695733)
XLA Ops:
  0.0 97.6 %shard_map.100 = f32[4,128]{1,0:T(4,128)} custom-call(s32[4]{0:T(128)} %tlen_in.1, s32[4]{0:T(128)} %vlen_in.1, bf16[1376,128]{1,0:T(8,128)(2,1)} %bitcast.3, bf16[1376,128]{1,0:T(8,128)(2,1)} %bitcast.4, bf16[256,512]{1,0:T(8,128)(2,1)} %tacts.1, bf16[256,512]{1,0:T(8,128)(2,1)} %vacts.1, bf16[256,512]{1,0:T(8,128)(2,1)} %tcot.1, bf16[256,512]{1,0:T(8,128)(2,1)} %vcot.1, ...), custom_call_target="tpu_custom_call" | custom-call | tf_op jit(solution)/shard_map/pallas_call | solution.py:491
  97.6 1.3 %copy.12 = f32[4,128]{1,0:T(4,128)} copy(f32[4,128]{1,0:T(4,128)} %shard_map.100) | data formatting | bytes 4096
